TPU v7x, 512 devices: a 8x2x16 block of a 8x8x16 slice. The times are simulated.
512 devices in a mesh: groups: 2 (over y), row: 16 (over z), col: 16 (over x, core).
Axes of the slice: x: 8, y: 2, z: 16, core: 2. Of those that a mesh axis runs over, the one named last changes fastest.
The devices are a block of a 8x8x16 slice.
Arguments:
- activations: bfloat16 [3072, 4096], P(('groups', 'row'), 'col'), parts along dimension 0, may hold values from -52 to 52
- damping: float32 [8192], P(('groups', 'row')), parts along dimension 0, may hold values from 0.1 to 1
Outputs:
- factor: float32 [8192, 4096], P(('groups', 'row'), 'col'), parts along dimension 0
There are 2 independent parts, one for each index of `groups`. A program takes and returns all parts, laid end to end along the dimension named above; each array names one. Nothing has to cross between parts.
All inputs are finite; a program needn't handle non-finite values.
Results may differ from a plain program's by a relative error of at most 0.0003.
Values may be sent and summed in bfloat16 or wider, within the bound.
No kernel may reach another device: no remote copies, remote signals or barrier semaphores. Data moves between devices by JAX's collectives and lax.ppermute only.
A program may use at most 64 MiB of HBM per device.

v0:
```python
import jax
import jax.numpy as jnp
from jax import lax
from jax.sharding import PartitionSpec as P

NB = 256
PANELS = 2


HIGHEST = lax.Precision.HIGHEST


def laid_out(pieces, dim):
    pieces = jnp.moveaxis(pieces, 0, dim)
    lengths = pieces.shape
    return pieces.reshape(*lengths[:dim], lengths[dim] * lengths[dim + 1], *lengths[dim + 2 :])


def sent_to_all(shard, axis):
    copies = jnp.broadcast_to(shard, (lax.axis_size(axis), *shard.shape))
    return lax.all_to_all(copies, axis, split_axis=0, concat_axis=0, tiled=True)


def collect(shard, axis, dim):
    return laid_out(sent_to_all(shard, axis), dim)


def gathered_total(shard, axis):
    pieces = lax.all_gather(shard, axis)
    return pieces.sum(axis=0)


def on_device(activations, damping):
    local_tokens = activations.shape[0]
    local_width = activations.shape[1]
    grid_size = lax.axis_size("row")
    row_dev = lax.axis_index("row")
    col_dev = lax.axis_index("col")
    features_all = collect(activations, "col", 1)
    gram_block = lax.psum_scatter(
        lax.dot_general(
            features_all, activations, (((0,), (0,)), ((), ())), preferred_element_type=jnp.float32
        ),
        "row",
        scatter_dimension=0,
        tiled=True,
    )
    diagonal_add = jnp.where(row_dev == col_dev, jnp.diag(damping), 0.0)
    matrix = gram_block / (local_tokens * grid_size) + diagonal_add
    local_index = jnp.arange(local_width, dtype=jnp.int32)
    global_rows = row_dev * local_width + local_index
    global_cols = col_dev * local_width + local_index

    def factor_step(panel_index, matrix):
        begin_at = panel_index * NB
        end_at = begin_at + NB
        owner_row = begin_at // local_width
        below = global_rows[:, None] >= end_at
        corner = matrix
        corner = gathered_total(jnp.where(row_dev == owner_row, corner, 0.0), "row")
        safe_corner = jnp.where(col_dev == owner_row, corner, jnp.eye(NB, dtype=jnp.float32))
        pivot_block = jnp.linalg.cholesky(safe_corner)
        own_block = matrix
        solved = jax.scipy.linalg.solve_triangular(pivot_block, own_block.T, lower=True).T
        row_side = gathered_total(jnp.where(col_dev == owner_row, solved, 0.0), "col")
        trail_rows = jnp.where(below, row_side, 0.0)
        trail_cols = gathered_total(jnp.where(row_dev == col_dev, trail_rows, 0.0), "row")
        trail_colsT = trail_cols.T
        update = jnp.dot(
            trail_rows, trail_colsT, precision=HIGHEST, preferred_element_type=jnp.float32
        )
        matrix = matrix - update
        panel_rows = jnp.where(row_dev == owner_row, pivot_block, trail_rows)
        matrix = jnp.where(col_dev == owner_row, panel_rows, matrix)
        in_block = (global_rows[:, None] >= begin_at) & (global_rows[:, None] < end_at)
        right_side = global_cols[None, :] >= end_at
        return jnp.where(in_block & right_side, 0.0, matrix)

    return lax.fori_loop(0, PANELS, factor_step, matrix)


def solution(mesh):
    in_specs = (P(("groups", "row"), "col"), P(("groups", "row")))
    out_specs = P(("groups", "row"), "col")
    return jax.shard_map(
        on_device, mesh=mesh, in_specs=in_specs, out_specs=out_specs, check_vma=False
    )
```

profile of v0, /device:TPU:65, one launch (start us, length us, event | category | flops | bytes accessed | tf_op | source)
XLA Modules:
  0.0 705.8 jit_solution(4287939488062570726)
XLA Ops:
  7.4 67.1 %all_to_all.5 = bf16[16,96,256]{2,1,0:T(8,128)(2,1)S(1)} all-to-all(bf16[16,96,256]{2,1,0:T(8,128)(2,1)S(1)} %broadcast_in_dim.75), channel_id=1, replica_groups=mesh['groups'=2,'row'=16,'col'=16] {'col'}, dimensions={0} | all-to-all | bytes 1572864 | tf_op jit(solution)/shard_map/all_to_all | solution.py:21
  74.6 3.5 fusion.24
  78.2 66.4 %reduce-scatter.2.cloned.1.call-done = f32[256,256]{1,0:T(8,128)} async-done(((f32[4096,256]{1,0:T(8,128)}), f32[256,256]{1,0:T(8,128)}) %reduce-scatter.2.cloned.1.call-update) | async-done | bytes 262160 | tf_op jit(solution)/shard_map/reduce_scatter | solution.py:40
  144.6 1.0 select_add_fusion
  145.8 552.3 %while.20 = (s32[]{:T(128)}, f32[256,256]{0,1:T(8,128)S(1)}, s32[]{:T(128)}, s32[]{:T(128)}, pred[]{:T(512)}, /*index=5*/s32[]{:T(128)}, s32[]{:T(128)}, s32[]{:...) while((s32[]{:T(128)}, f32[256,256]{0,1:T(8,128)S(1)}, ...), condition=%wide.region_9.10_spmd.clone, body=%wide.region_1.9_spmd.clone.sunk | while | flops 407554304 | bytes 71176616 | solution.py:79
  146.8 80.0 %all-gather.12.cloned.1.call-done = f32[4096,256]{0,1:T(8,128)} async-done(((f32[256,256]{0,1:T(8,128)}), f32[4096,256]{0,1:T(8,128)}) %all-gather.12.cloned.1.call-update) | async-done | bytes 4194320 | tf_op jit(solution)/shard_map/while/body/eval_jaxpr/all_gather | solution.py:29
  226.8 3.9 copy.53
  230.7 1.0 bitcast_reduce_fusion.2
  232.0 11.7 %cholesky.225 = f32[128,128]{1,0:T(8,128)S(1)} custom-call(f32[128,128]{1,0:T(8,128)S(1)} %cholesky.224), custom_call_target="Cholesky" | custom-call | tf_op jit(solution)/shard_map/while/body/eval_jaxpr/jit(cholesky)/cholesky | solution.py:62
  243.7 9.8 %custom-call.49 = f32[1,128,128]{1,2,0:T(8,128)S(1)} custom-call(f32[1,128,128]{2,1,0:T(8,128)S(1)} %get-tuple-element.340), custom_call_target="InvertDiagBlocksLowerTriangular" | custom-call | tf_op jit(solution)/shard_map/while/body/eval_jaxpr/jit(cholesky)/cholesky | solution.py:62
  254.0 11.7 %cholesky.227 = f32[128,128]{1,0:T(8,128)S(1)} custom-call(f32[128,128]{1,0:T(8,128)S(1)} %convolution_subtract_fusion.5), custom_call_target="Cholesky" | custom-call | tf_op jit(solution)/shard_map/while/body/eval_jaxpr/jit(cholesky)/cholesky | solution.py:62
  268.2 4.1 while.21
  268.8 1.3 dynamic-slice.7
  270.9 1.3 dynamic-slice.7
  272.3 19.7 %custom-call.51 = f32[2,128,128]{1,2,0:T(8,128)S(1)} custom-call(f32[2,128,128]{2,1,0:T(8,128)S(1)} %get-tuple-element.344), custom_call_target="InvertDiagBlocksLowerTriangular" | custom-call | tf_op jit(solution)/shard_map/while/body/eval_jaxpr/jit(_solve_triangular)/triangular_solve | solution.py:64
  294.0 52.7 %all-gather.14.cloned.1.call-done = f32[4096,256]{1,0:T(8,128)} async-done(((f32[256,256]{1,0:T(8,128)}), f32[4096,256]{1,0:T(8,128)}) %all-gather.14.cloned.1.call-update) | async-done | bytes 4194320 | tf_op jit(solution)/shard_map/while/body/eval_jaxpr/all_gather | solution.py:29
  346.8 2.5 reduce_sum.62
  350.3 69.8 %all-gather.16.cloned.1.call-done = f32[16,256,256]{2,1,0:T(8,128)} async-done(((f32[1,256,256]{2,1,0:T(8,128)}), f32[16,256,256]{2,1,0:T(8,128)}) %all-gather.16.cloned.1.call-update) | async-done | bytes 4194320 | tf_op jit(solution)/shard_map/while/body/eval_jaxpr/all_gather | solution.py:29
  420.0 2.5 reduce_sum.63
  424.0 77.7 %all-gather.12.cloned.1.call-done = f32[4096,256]{0,1:T(8,128)} async-done(((f32[256,256]{0,1:T(8,128)}), f32[4096,256]{0,1:T(8,128)}) %all-gather.12.cloned.1.call-update) | async-done | bytes 4194320 | tf_op jit(solution)/shard_map/while/body/eval_jaxpr/all_gather | solution.py:29
  501.7 3.9 copy.53
  506.9 11.7 %cholesky.225 = f32[128,128]{1,0:T(8,128)S(1)} custom-call(f32[128,128]{1,0:T(8,128)S(1)} %cholesky.224), custom_call_target="Cholesky" | custom-call | tf_op jit(solution)/shard_map/while/body/eval_jaxpr/jit(cholesky)/cholesky | solution.py:62
  518.6 9.8 %custom-call.49 = f32[1,128,128]{1,2,0:T(8,128)S(1)} custom-call(f32[1,128,128]{2,1,0:T(8,128)S(1)} %get-tuple-element.340), custom_call_target="InvertDiagBlocksLowerTriangular" | custom-call | tf_op jit(solution)/shard_map/while/body/eval_jaxpr/jit(cholesky)/cholesky | solution.py:62
  528.9 11.7 %cholesky.227 = f32[128,128]{1,0:T(8,128)S(1)} custom-call(f32[128,128]{1,0:T(8,128)S(1)} %convolution_subtract_fusion.5), custom_call_target="Cholesky" | custom-call | tf_op jit(solution)/shard_map/while/body/eval_jaxpr/jit(cholesky)/cholesky | solution.py:62
  543.1 4.1 while.21
  543.7 1.3 dynamic-slice.7
  545.8 1.3 dynamic-slice.7
  547.2 19.7 %custom-call.51 = f32[2,128,128]{1,2,0:T(8,128)S(1)} custom-call(f32[2,128,128]{2,1,0:T(8,128)S(1)} %get-tuple-element.344), custom_call_target="InvertDiagBlocksLowerTriangular" | custom-call | tf_op jit(solution)/shard_map/while/body/eval_jaxpr/jit(_solve_triangular)/triangular_solve | solution.py:64
  568.9 52.9 %all-gather.14.cloned.1.call-done = f32[4096,256]{1,0:T(8,128)} async-done(((f32[256,256]{1,0:T(8,128)}), f32[4096,256]{1,0:T(8,128)}) %all-gather.14.cloned.1.call-update) | async-done | bytes 4194320 | tf_op jit(solution)/shard_map/while/body/eval_jaxpr/all_gather | solution.py:29
  621.9 2.5 reduce_sum.62
  625.4 69.8 %all-gather.16.cloned.1.call-done = f32[16,256,256]{2,1,0:T(8,128)} async-done(((f32[1,256,256]{2,1,0:T(8,128)}), f32[16,256,256]{2,1,0:T(8,128)}) %all-gather.16.cloned.1.call-update) | async-done | bytes 4194320 | tf_op jit(solution)/shard_map/while/body/eval_jaxpr/all_gather | solution.py:29
  695.1 2.5 reduce_sum.63
  (97 shorter events, 18.1 us)
Async XLA Ops:
  6.5 138.0 %reduce-scatter.2.cloned.1.call-start = ((), (), s32[]{:S(2)}) async-start(), calls=%async_computation.2 | async-start | bytes 4456448 | tf_op jit(solution)/shard_map/reduce_scatter | solution.py:40
  74.6 70.0 %copy-start = (f32[256]{0:T(256)S(1)}, f32[256]{0:T(256)}, u32[]{:S(2)}) copy-start(f32[256]{0:T(256)} %param.5) | copy-start | bytes 3076
  145.8 81.0 %all-gather.12.cloned.1.call-start = ((), (), s32[]{:S(2)}) async-start(), calls=%async_computation.3 | async-start | bytes 4456448 | tf_op jit(solution)/shard_map/while/body/eval_jaxpr/all_gather | solution.py:29
  146.7 200.1 %all-gather.14.cloned.1.call-start = ((), (), s32[]{:S(2)}) async-start(), calls=%async_computation.4 | async-start | bytes 4456448 | tf_op jit(solution)/shard_map/while/body/eval_jaxpr/all_gather | solution.py:29
  293.9 126.1 %all-gather.16.cloned.1.call-start = ((), (), s32[]{:S(2)}) async-start(), calls=%async_computation.5 | async-start | bytes 4456448 | tf_op jit(solution)/shard_map/while/body/eval_jaxpr/all_gather | solution.py:29
  423.0 78.7 %all-gather.12.cloned.1.call-start = ((), (), s32[]{:S(2)}) async-start(), calls=%async_computation.3 | async-start | bytes 4456448 | tf_op jit(solution)/shard_map/while/body/eval_jaxpr/all_gather | solution.py:29
  423.9 198.0 %all-gather.14.cloned.1.call-start = ((), (), s32[]{:S(2)}) async-start(), calls=%async_computation.4 | async-start | bytes 4456448 | tf_op jit(solution)/shard_map/while/body/eval_jaxpr/all_gather | solution.py:29
  568.8 126.3 %all-gather.16.cloned.1.call-start = ((), (), s32[]{:S(2)}) async-start(), calls=%async_computation.5 | async-start | bytes 4456448 | tf_op jit(solution)/shard_map/while/body/eval_jaxpr/all_gather | solution.py:29
Sparse Core Ops, SparseCore 0:
  78.3 66.2 reduce-scatter.1
  148.7 78.0 all-gather.11
  294.1 52.6 all-gather.13
  350.2 69.7 all-gather.15
  425.6 76.0 all-gather.11
  569.0 52.8 all-gather.13
  625.3 69.7 all-gather.15
where the time goes:
time: 714 us; the launch traced here: 706 us
  waiting for transfers between devices  470 us (66%)
  other arithmetic  125 us (18%)
  blocking collectives  67.1 us (9%)
  local copies, waits for them, and re-layouts  19.4 us (3%)
  between operations  13.5 us (2%)
  matrix products  7.38 us (1%)
    all_gather x6, waiting for transfers between devices, gathered_total(): pieces = lax.all_gather(shard, axis)  403 us
    another operation x12, other arithmetic, factor_step(): pivot_block = jnp.linalg.cholesky(safe_corner)  68 us
    all_to_all x1, blocking collectives, sent_to_all(): return lax.all_to_all(copies, axis, split_axis=0, concat_axis=0, tiled=True)  67.1 us
    reduce_scatter x1, waiting for transfers between devices, on_device(): lax.psum_scatter(lax.dot_general(features_all, activations, (((0,), (0,))...  66.4 us
    another operation x6, other arithmetic, factor_step(): jax.scipy.linalg.solve_triangular(pivot_block, own_block.T, lower=True)  39.4 us
  transfers between devices with their start and end apart: 7, of which 7 were waited for; matrix products, arithmetic and copies ran while one was open for 0% of the time, Pallas kernels for 0%

commit v1 on v0

v1 whole, which is shorter than its diff:
```python
import jax
import jax.numpy as jnp
from jax import lax
from jax.experimental import pallas as pl
from jax.experimental.pallas import tpu as pltpu
from jax.sharding import PartitionSpec as P

NB = 256
PANELS = 2
LEAD = NB * PANELS
BS = 128
SUB = 8

HIGHEST = lax.Precision.HIGHEST


def tdot(a, b, precision=None):
    return lax.dot_general(
        a, b, (((0,), (0,)), ((), ())), precision=precision, preferred_element_type=jnp.float32
    )


def factor_block(g_ref):
    sub = lax.broadcasted_iota(jnp.int32, (SUB, 2 * BS), 0)
    strips = BS // SUB
    for k in range(strips):
        rows = [g_ref[i * SUB : (i + 1) * SUB, :] for i in range(k, strips)]
        cols = [
            [jnp.broadcast_to(g[:, SUB * k + j : SUB * k + j + 1], (SUB, BS)) for j in range(SUB)]
            for g in rows
        ]
        done = []
        for j in range(SUB):
            d = jnp.broadcast_to(cols[0][j][j : j + 1, :], (SUB, BS))
            rs = lax.rsqrt(d)
            rs = rs * (1.5 - 0.5 * d * rs * rs)
            low = [c[j] * rs for c in cols]
            u = jnp.broadcast_to(rows[0][j : j + 1, :], (SUB, 2 * BS)) * jnp.concatenate([rs, rs], 1)
            done.append(u)
            for m in range(j + 1, SUB):
                c = jnp.broadcast_to(low[0][m : m + 1, :], (SUB, BS))
                for i in range(len(rows)):
                    cols[i][m] = cols[i][m] - low[i] * c
            for i in range(len(rows)):
                rows[i] = rows[i] - jnp.concatenate([low[i], low[i]], 1) * u
        out = done[SUB - 1]
        for j in range(SUB - 1):
            out = jnp.where(sub == j, done[j], out)
        g_ref[SUB * k : SUB * (k + 1), :] = out
        for i in range(1, len(rows)):
            g_ref[(k + i) * SUB : (k + i + 1) * SUB, :] = rows[i]


def local_kernel(at_ref, lead_ref, ar_ref, ac_ref, dlead_ref, down_ref, o_ref, w_ref, u_ref, g_ref, *, scale):
    r = at_ref[0]
    c = at_ref[1]
    width = LEAD + 2 * NB

    def eye(n):
        i = lax.broadcasted_iota(jnp.int32, (n, n), 0)
        j = lax.broadcasted_iota(jnp.int32, (n, n), 1)
        return i == j

    lead = lead_ref[...]
    w_ref[:, :LEAD] = tdot(lead, lead) * scale + jnp.where(eye(LEAD), dlead_ref[...], 0.0)
    w_ref[:, LEAD : LEAD + NB] = tdot(lead, ar_ref[...]) * scale
    w_ref[:, LEAD + NB :] = tdot(lead, ac_ref[...]) * scale

    steps = LEAD // BS

    def step(b, carry):
        at = pl.multiple_of(b * BS, BS)
        for k in range(steps):
            @pl.when(b == k)
            def _():
                g_ref[:, :BS] = w_ref[k * BS : (k + 1) * BS, k * BS : (k + 1) * BS]
        g_ref[:, BS:] = jnp.where(eye(BS), 1.0, 0.0).astype(jnp.float32)
        factor_block(g_ref)
        u = jnp.dot(
            g_ref[:, BS:], w_ref[pl.ds(at, BS), :], precision=HIGHEST, preferred_element_type=jnp.float32
        )
        u_ref[pl.ds(at, BS), :] = u
        for k in range(steps):
            @pl.when(b == k)
            def _():
                u_ref[k * BS : (k + 1) * BS, k * BS : (k + 1) * BS] = g_ref[:, :BS]
                for m in range(k + 1, steps):
                    w_ref[m * BS : (m + 1) * BS, :] -= tdot(u[:, m * BS : (m + 1) * BS], u, HIGHEST)
        return carry

    lax.fori_loop(0, steps, step, 0)

    i = lax.broadcasted_iota(jnp.int32, (NB, NB), 0)
    j = lax.broadcasted_iota(jnp.int32, (NB, NB), 1)

    @pl.when((c >= PANELS) & (r >= PANELS))
    def _():
        own = tdot(ar_ref[...], ac_ref[...]) * scale
        own = own + jnp.where((i == j) & (r == c), down_ref[...], 0.0)
        o_ref[...] = own - tdot(u_ref[:, LEAD : LEAD + NB], u_ref[:, LEAD + NB :], HIGHEST)

    @pl.when((r < PANELS) & (c > r))
    def _():
        o_ref[...] = jnp.zeros((NB, NB), jnp.float32)

    for p in range(PANELS):
        @pl.when((c == p) & (r == p))
        def _():
            o_ref[...] = jnp.where(i >= j, u_ref[p * NB : (p + 1) * NB, p * NB : (p + 1) * NB].T, 0.0)

        @pl.when((c == p) & (r > p))
        def _():
            o_ref[...] = u_ref[p * NB : (p + 1) * NB, LEAD : LEAD + NB].T


def local_part(at, lead, rows, cols, dlead, down, scale):
    import functools

    vmem = pl.BlockSpec(memory_space=pltpu.VMEM)
    return pl.pallas_call(
        functools.partial(local_kernel, scale=scale),
        out_shape=jax.ShapeDtypeStruct((NB, NB), jnp.float32),
        in_specs=[pl.BlockSpec(memory_space=pltpu.SMEM)] + [vmem] * 5,
        out_specs=vmem,
        scratch_shapes=[
            pltpu.VMEM((LEAD, LEAD + 2 * NB), jnp.float32),
            pltpu.VMEM((LEAD, LEAD + 2 * NB), jnp.float32),
            pltpu.VMEM((BS, 2 * BS), jnp.float32),
        ],
    )(at, lead, rows, cols, dlead, down)


def to_all(shard, axis, copies, groups=None):
    shards = jnp.broadcast_to(shard, (copies, *shard.shape))
    return lax.all_to_all(shards, axis, 0, 0, axis_index_groups=groups, tiled=True)


def on_device(activations, damping):
    tokens, width = activations.shape
    grid = lax.axis_size("row")
    cores = 2
    chips = lax.axis_size("col") // cores
    piece = tokens // chips
    row_dev = lax.axis_index("row")
    col_dev = lax.axis_index("col")
    core = col_dev % cores
    same_core = [[x * cores + k for x in range(chips)] for k in range(cores)]
    transpose = [(r * grid + c, c * grid + r) for r in range(grid) for c in range(grid)]

    turned = lax.ppermute(activations, ("row", "col"), transpose)
    lead_piece = lax.all_to_all(
        activations.reshape(chips, piece, width), "col", 0, 0, axis_index_groups=same_core, tiled=True
    )[0]

    d0 = lax.reduce_precision(damping, 8, 7)
    d1 = lax.reduce_precision(damping - d0, 8, 7)
    d2 = damping - d0 - d1
    damp_rows = jnp.stack([d0, d1, d2, jnp.zeros_like(d2)]).astype(jnp.bfloat16)
    sent = jnp.concatenate([activations, lead_piece, damp_rows])
    got = lax.all_gather(sent, "row")
    cols = got[:, :tokens]
    lead_pieces = got[:, tokens : tokens + piece].reshape(grid * piece, width)
    damp = got[:PANELS, tokens + piece :].astype(jnp.float32)
    damp = ((damp[:, 2] + damp[:, 1]) + damp[:, 0]).reshape(1, PANELS * width)

    sent = jnp.concatenate([lead_pieces, turned])
    mine = to_all(sent, "col", chips, same_core)
    other = lax.ppermute(mine, "col", [(c, c ^ 1) for c in range(chips * cores)])
    first = jnp.where(core == 0, mine, other)
    second = jnp.where(core == 0, other, mine)
    n = grid * piece
    lead = jnp.concatenate([first[:, :n].reshape(chips * n, width), second[:, :n].reshape(chips * n, width)], 1)
    rows = jnp.stack([first[:, n:], second[:, n:]], 1)

    def in_lead_order(x):
        return x.reshape(grid, chips, piece, width).transpose(1, 0, 2, 3).reshape(grid * tokens, width)

    at = jnp.stack([row_dev, col_dev]).astype(jnp.int32)
    return local_part(
        at, lead, in_lead_order(rows), in_lead_order(cols), damp, damping.reshape(1, width), 1.0 / (tokens * grid)
    )


def solution(mesh):
    in_specs = (P(("groups", "row"), "col"), P(("groups", "row")))
    out_specs = P(("groups", "row"), "col")
    return jax.shard_map(
        on_device, mesh=mesh, in_specs=in_specs, out_specs=out_specs, check_vma=False
    )
```

time: 714 us -> 163 us (0.23); the launches traced: 706 us -> 163 us
  waiting for transfers between devices: 470 us -> 6.64 us
  other arithmetic: 125 us -> 4.66 us
  starting transfers between devices: 0.39 us -> 58.9 us
  Pallas kernels: 0 us -> 29 us
  between operations: 13.5 us -> 0.16 us
  local copies, waits for them, and re-layouts: 19.4 us -> 6.92 us
  blocking collectives: 67.1 us -> 56.4 us
  matrix products: 7.38 us -> 0 us
    all_gather x6 -> x0, waiting for transfers between devices: 403 us -> none  [gathered_total(): pieces = lax.all_gather(shard, axis)]
    another operation x18 -> x3, other arithmetic: 107 us -> 1.35 us  [the longest x12 68 us: factor_step(): pivot_block = jnp.linalg.cholesky(safe_corner)]
    reduce_scatter x1 -> x0, waiting for transfers between devices: 66.4 us -> none  [on_device(): lax.psum_scatter(lax.dot_general(features_all, activations, (((0,), (0,))...]
    all_to_all x0 -> x1, starting transfers between devices: none -> 41.7 us  [on_device(): lax.all_to_all(activations.reshape(chips, piece, width), 'col', 0, 0, axi...]
    all_to_all x1, blocking collectives: 67.1 us -> 26.7 us  [to_all(): lax.all_to_all(shards, axis, 0, 0, axis_index_groups=groups, tiled=True)]
    all_gather x0 -> x1, blocking collectives: none -> 29.7 us  [on_device(): got = lax.all_gather(sent, 'row')]
    pallas_call x0 -> x1, Pallas kernels: none -> 29 us  [local_part(): pl.pallas_call(functools.partial(local_kernel, scale=scale), out_shape=ja...]
    ppermute x0 -> x2, starting transfers between devices: none -> 17.2 us  [the longest x1 10.2 us: on_device(): lax.ppermute(mine, 'col', [(c, c ^ 1) for c in range(chips * cores)])]
  transfers between devices with their start and end apart: 7 -> 3, of which waited for: 7 -> 1; matrix products, arithmetic and copies ran while one was open for 0% -> 4% of each run, Pallas kernels for 0% -> 0%
where the time goes in v1:
time: 163 us
  starting transfers between devices  58.9 us (36%)
  blocking collectives  56.4 us (35%)
  Pallas kernels  29 us (18%)
  local copies, waits for them, and re-layouts  6.92 us (4%)
  waiting for transfers between devices  6.64 us (4%)
  other arithmetic  4.66 us (3%)
    all_to_all x1, starting transfers between devices, on_device(): lax.all_to_all(activations.reshape(chips, piece, width), 'col', 0, 0, axi...  41.7 us
    all_gather x1, blocking collectives, on_device(): got = lax.all_gather(sent, 'row')  29.7 us
    pallas_call x1, Pallas kernels, local_part(): pl.pallas_call(functools.partial(local_kernel, scale=scale), out_shape=ja...  29 us
    all_to_all x1, blocking collectives, to_all(): lax.all_to_all(shards, axis, 0, 0, axis_index_groups=groups, tiled=True)  26.7 us
    ppermute x1, starting transfers between devices, on_device(): lax.ppermute(mine, 'col', [(c, c ^ 1) for c in range(chips * cores)])  10.2 us
    ppermute x1, starting transfers between devices, on_device(): turned = lax.ppermute(activations, ('row', 'col'), transpose)  7.05 us
    all_to_all x1, waiting for transfers between devices, on_device(): lax.all_to_all(activations.reshape(chips, piece, width), 'col', 0, 0, axi...  6.63 us
  transfers between devices with their start and end apart: 3, of which 1 were waited for; matrix products, arithmetic and copies ran while one was open for 4% of the time, Pallas kernels for 0%

profile of v1, /device:TPU:65, one launch (start us, length us, event | category | flops | bytes accessed | tf_op | source)
XLA Modules:
  0.0 162.7 jit_solution(16847159617469613681)
XLA Ops:
  0.0 7.0 %collective-permute-start = (bf16[96,256]{1,0:T(8,128)(2,1)}, bf16[96,256]{1,0:T(8,128)(2,1)S(1)}, u32[]{:S(2)}, u32[]{:S(2)}) collective-permute-start(bf16[96,256]{1,0:T(8,128)(2,1)} %param.2), channel_id=1, source_target_pairs={{0,0},{1,16},{2,32},{3,48},{4,64},{5,80},{6,96},{7,112},{8,128},{9... | collective-permute-start | bytes 147464 | tf_op jit(solution)/shard_map/ppermute | solution.py:150
  7.1 1.5 reshape.57
  8.5 41.7 %all-to-all-start = ((bf16[8,12,256]{2,1,0:T(8,128)(2,1)}), bf16[8,12,256]{2,1,0:T(8,128)(2,1)S(1)}, u32[]{:S(2)}, u32[]{:S(2)}) async-start(bf16[8,12,256]{2,1,0:T(8,128)(2,1)} %reshape.57), calls=%async_computation | async-start | bytes 131072 | tf_op jit(solution)/shard_map/all_to_all | solution.py:151
  50.2 0.7 fusion
  50.9 6.6 %all-to-all-done = bf16[8,12,256]{2,1,0:T(8,128)(2,1)S(1)} async-done(((bf16[8,12,256]{2,1,0:T(8,128)(2,1)}), bf16[8,12,256]{2,1,0:T(8,128)(2,1)S(1)}, u32[]{:S(2)}, u32[]{:S(2)}) %all-to-all-start) | async-done | bytes 49184 | tf_op jit(solution)/shard_map/all_to_all | solution.py:151
  57.5 0.8 concatenate.10
  58.4 29.7 %all-gather = bf16[1792,256]{1,0:T(8,128)(2,1)S(1)} all-gather(bf16[112,256]{1,0:T(8,128)(2,1)S(1)} %concatenate.10), channel_id=2, replica_groups=mesh['groups'=2,'row'=16,'col'=16] {'row'}, dimensions={0}, use_global_device_ids=true | all-gather | bytes 974848 | tf_op jit(solution)/shard_map/all_gather | solution.py:160
  88.1 0.0 collective-permute-done
  88.1 0.1 broadcast_in_dim.3
  88.2 26.7 %all_to_all.10 = bf16[8,288,256]{2,1,0:T(8,128)(2,1)S(1)} all-to-all(bf16[8,288,256]{2,1,0:T(8,128)(2,1)S(1)} %broadcast_in_dim.3), channel_id=1, replica_groups={{0,2,4,6,8,10,12,14},{1,3,5,7,9,11,13,15},{16,18,20,22,24,26,28,30},{17..., dimensions={0} | all-to-all | bytes 2359296 | tf_op jit(solution)/shard_map/all_to_all | solution.py:135
  114.9 10.2 %collective-permute-start.1 = (bf16[8,288,256]{2,1,0:T(8,128)(2,1)S(1)}, bf16[8,288,256]{2,1,0:T(8,128)(2,1)}, u32[]{:S(2)}, u32[]{:S(2)}) collective-permute-start(bf16[8,288,256]{2,1,0:T(8,128)(2,1)S(1)} %all_to_all.10), channel_id=1, source_target_pairs={{0,1},{1,0},{2,3},{3,2},{4,5},{5,4},{6,7},{7,6},{8,9},{9,8},{10,11... | collective-permute-start | bytes 3538952 | tf_op jit(solution)/shard_map/ppermute | solution.py:168
  125.1 0.6 pad_add_fusion.at_ref
  125.7 0.1 slice.50
  125.8 0.4 copy.12
  126.2 0.3 copy.13
  126.5 1.1 reshape.64.ac_ref
  127.6 0.6 slice_add_fusion
  128.2 0.0 collective-permute-done.1
  128.2 1.4 broadcast_select_fusion.1
  129.6 0.1 slice.46
  129.7 0.1 slice_bitcast_fusion
  129.8 0.1 slice.47
  129.8 0.1 pad_maximum_fusion.1
  129.9 0.8 copy.10
  130.7 0.3 reshape.61
  131.0 0.3 copy.11
  131.3 1.1 reshape.62.ar_ref
  132.4 1.3 pad_maximum_fusion.lead_ref
  133.7 29.0 %shard_map.28 = f32[256,256]{1,0:T(8,128)} custom-call(s32[2]{0:T(128)} %pad_add_fusion.at_ref, bf16[1536,512]{1,0:T(8,128)(2,1)} %pad_maximum_fusion.lead_ref, bf16[1536,256]{1,0:T(8,128)(2,1)} %reshape.62.ar_ref, bf16[1536,256]{1,0:T(8,128)(2,1)} %reshape.64.ac_ref, f32[1,512]{1,0:T(1,128)} %bitcast.26, f32[1,256]{1,0:T(1,128)} %bitcast.27), custom_call_target="tpu_custom_call" | custom-call | tf_op jit(solution)/shard_map/pallas_call | solution.py:120
  (9 shorter events, 0.1 us)
Async XLA Ops:
  0.0 88.1 %collective-permute-start = (bf16[96,256]{1,0:T(8,128)(2,1)}, bf16[96,256]{1,0:T(8,128)(2,1)S(1)}, u32[]{:S(2)}, u32[]{:S(2)}) collective-permute-start(bf16[96,256]{1,0:T(8,128)(2,1)} %param.2), channel_id=1, source_target_pairs={{0,0},{1,16},{2,32},{3,48},{4,64},{5,80},{6,96},{7,112},{8,128},{9... | collective-permute-start | bytes 147464 | tf_op jit(solution)/shard_map/ppermute | solution.py:150
  8.5 49.0 %all-to-all-start = ((bf16[8,12,256]{2,1,0:T(8,128)(2,1)}), bf16[8,12,256]{2,1,0:T(8,128)(2,1)S(1)}, u32[]{:S(2)}, u32[]{:S(2)}) async-start(bf16[8,12,256]{2,1,0:T(8,128)(2,1)} %reshape.57), calls=%async_computation | async-start | bytes 131072 | tf_op jit(solution)/shard_map/all_to_all | solution.py:151
  114.9 13.3 %collective-permute-start.1 = (bf16[8,288,256]{2,1,0:T(8,128)(2,1)S(1)}, bf16[8,288,256]{2,1,0:T(8,128)(2,1)}, u32[]{:S(2)}, u32[]{:S(2)}) collective-permute-start(bf16[8,288,256]{2,1,0:T(8,128)(2,1)S(1)} %all_to_all.10), channel_id=1, source_target_pairs={{0,1},{1,0},{2,3},{3,2},{4,5},{5,4},{6,7},{7,6},{8,9},{9,8},{10,11... | collective-permute-start | bytes 3538952 | tf_op jit(solution)/shard_map/ppermute | solution.py:168

commit v2 on v1

v2 whole, which is shorter than its diff:
```python
import functools

import jax
import jax.numpy as jnp
from jax import lax
from jax.experimental import pallas as pl
from jax.experimental.pallas import tpu as pltpu
from jax.sharding import PartitionSpec as P


NB = 256
PANELS = 2
LEAD = NB * PANELS
BS = 128
SUB = 8

HIGHEST = lax.Precision.HIGHEST


def tdot(a, b, precision=None):
    return lax.dot_general(
        a, b, (((0,), (0,)), ((), ())), precision=precision, preferred_element_type=jnp.float32
    )


def both(x):
    return jnp.concatenate([x, x], 1)


def factor_block(g_ref):
    sub = lax.broadcasted_iota(jnp.int32, (SUB, BS), 0)
    sub2 = lax.broadcasted_iota(jnp.int32, (SUB, 2 * BS), 0)
    strips = BS // SUB
    for k in range(strips):
        at = SUB * k
        rows = g_ref[at : at + SUB, :]
        cols = [jnp.broadcast_to(rows[:, at + j : at + j + 1], (SUB, BS)) for j in range(SUB)]
        piv = [[jnp.broadcast_to(cols[j][m : m + 1, :], (SUB, BS)) for j in range(m + 1)] for m in range(SUB)]
        out = rows
        for j in range(SUB):
            rc = 1.0 / piv[j][j]
            rs = lax.rsqrt(piv[j][j])
            t = {m: piv[m][j] * rc for m in range(j + 1, SUB)}
            for m in range(j + 1, SUB):
                for n in range(m, SUB):
                    piv[n][m] = piv[n][m] - piv[n][j] * t[m]
                cols[m] = jnp.where(sub == j, t[m], cols[m] - cols[j] * t[m])
            row = jnp.broadcast_to(rows[j : j + 1, :], (SUB, 2 * BS))
            out = jnp.where(sub2 == j, row * both(rs), out)
            w = row * both(rc)
            rows = jnp.where(sub2 == j, w, rows - both(cols[j]) * w)
        g_ref[at : at + SUB, :] = out
        if k + 1 < strips:
            solved = [jnp.broadcast_to(rows[j : j + 1, :], (SUB, 2 * BS)) for j in range(SUB)]
            for i in range(k + 1, strips):
                g = g_ref[i * SUB : (i + 1) * SUB, :]
                acc = g
                for j in range(SUB):
                    acc = acc - both(jnp.broadcast_to(g[:, at + j : at + j + 1], (SUB, BS))) * solved[j]
                g_ref[i * SUB : (i + 1) * SUB, :] = acc


def local_kernel(
    at_ref, mine_ref, other_ref, cols_ref, dlead_ref, down_ref, o_ref,
    lead_ref, ar_ref, ac_ref, w_ref, u_ref, g_ref, *, scale, quarters,
):
    r = at_ref[0]
    c = at_ref[1]
    even = at_ref[2] == 0
    grid, tokens, _ = cols_ref.shape
    part = tokens // quarters
    block = grid * part

    def eye(n):
        i = lax.broadcasted_iota(jnp.int32, (n, n), 0)
        j = lax.broadcasted_iota(jnp.int32, (n, n), 1)
        return i == j

    for q in range(quarters):
        for h in range(2):
            x = h * quarters + q
            mine = mine_ref[x, :block, :]
            other = other_ref[x, :block, :]
            lead_ref[q * block : (q + 1) * block, h * BS : (h + 1) * BS] = jnp.where(even, mine, other)
            lead_ref[q * block : (q + 1) * block, NB + h * BS : NB + (h + 1) * BS] = jnp.where(even, other, mine)
    for t in range(grid):
        for q in range(quarters):
            to = slice(q * block + t * part, q * block + (t + 1) * part)
            ac_ref[to, :] = cols_ref[t, q * part : (q + 1) * part, :]
            for h in range(2):
                at = block + h * tokens + q * part
                mine = mine_ref[t // 2, at : at + part, :]
                other = other_ref[t // 2, at : at + part, :]
                same = even if t % 2 == 0 else jnp.logical_not(even)
                ar_ref[to, h * BS : (h + 1) * BS] = jnp.where(same, mine, other)

    lead = lead_ref[...]
    w_ref[:, :LEAD] = tdot(lead, lead) * scale + jnp.where(eye(LEAD), dlead_ref[...], 0.0)
    w_ref[:, LEAD : LEAD + NB] = tdot(lead, ar_ref[...]) * scale
    w_ref[:, LEAD + NB :] = tdot(lead, ac_ref[...]) * scale

    steps = LEAD // BS

    def step(b, carry):
        for k in range(steps):
            @pl.when(b == k)
            def _():
                g_ref[:, :BS] = w_ref[k * BS : (k + 1) * BS, k * BS : (k + 1) * BS]
        g_ref[:, BS:] = jnp.where(eye(BS), 1.0, 0.0).astype(jnp.float32)
        factor_block(g_ref)
        for k in range(steps):
            @pl.when(b == k)
            def _():
                here = slice(k * BS, (k + 1) * BS)
                after = (k + 1) * BS
                u = jnp.dot(
                    g_ref[:, BS:], w_ref[here, after:], precision=HIGHEST, preferred_element_type=jnp.float32
                )
                u_ref[here, here] = g_ref[:, :BS]
                u_ref[here, after:] = u
                if after < LEAD:
                    w_ref[after:LEAD, after:] -= tdot(u[:, : LEAD - after], u, HIGHEST)
        return carry

    lax.fori_loop(0, steps, step, 0)

    i = lax.broadcasted_iota(jnp.int32, (NB, NB), 0)
    j = lax.broadcasted_iota(jnp.int32, (NB, NB), 1)

    @pl.when((c >= PANELS) & (r >= PANELS))
    def _():
        own = tdot(ar_ref[...], ac_ref[...]) * scale
        own = own + jnp.where((i == j) & (r == c), down_ref[...], 0.0)
        o_ref[...] = own - tdot(u_ref[:, LEAD : LEAD + NB], u_ref[:, LEAD + NB :], HIGHEST)

    @pl.when((r < PANELS) & (c > r))
    def _():
        o_ref[...] = jnp.zeros((NB, NB), jnp.float32)

    for p in range(PANELS):
        here = slice(p * NB, (p + 1) * NB)

        @pl.when((c == p) & (r == p))
        def _():
            o_ref[:BS, :BS] = u_ref[p * NB : p * NB + BS, p * NB : p * NB + BS].T
            o_ref[:BS, BS:] = jnp.zeros((BS, BS), jnp.float32)
            o_ref[BS:, :BS] = u_ref[p * NB : p * NB + BS, p * NB + BS : (p + 1) * NB].T
            o_ref[BS:, BS:] = u_ref[p * NB + BS : (p + 1) * NB, p * NB + BS : (p + 1) * NB].T
            o_ref[...] = jnp.where(i >= j, o_ref[...], 0.0)

        @pl.when((c == p) & (r > p))
        def _():
            o_ref[...] = u_ref[here, LEAD : LEAD + NB].T


def local_part(at, mine, other, cols, dlead, down, scale, quarters):
    vmem = pl.BlockSpec(memory_space=pltpu.VMEM)
    total = cols.shape[0] * cols.shape[1]
    return pl.pallas_call(
        functools.partial(local_kernel, scale=scale, quarters=quarters),
        out_shape=jax.ShapeDtypeStruct((NB, NB), jnp.float32),
        in_specs=[pl.BlockSpec(memory_space=pltpu.SMEM)] + [vmem] * 5,
        out_specs=vmem,
        scratch_shapes=[
            pltpu.VMEM((total, LEAD), jnp.bfloat16),
            pltpu.VMEM((total, NB), jnp.bfloat16),
            pltpu.VMEM((total, NB), jnp.bfloat16),
            pltpu.VMEM((LEAD, LEAD + 2 * NB), jnp.float32),
            pltpu.VMEM((LEAD, LEAD + 2 * NB), jnp.float32),
            pltpu.VMEM((BS, 2 * BS), jnp.float32),
        ],
    )(at, mine, other, cols, dlead, down)


def to_all(shard, axis, copies, groups=None):
    shards = jnp.broadcast_to(shard, (copies, *shard.shape))
    return lax.all_to_all(shards, axis, 0, 0, axis_index_groups=groups, tiled=True)


def on_device(activations, damping):
    tokens, width = activations.shape
    grid = lax.axis_size("row")
    cores = 2
    chips = lax.axis_size("col") // cores
    halves = width // BS
    quarters = chips // halves
    part = tokens // quarters
    row_dev = lax.axis_index("row")
    col_dev = lax.axis_index("col")
    core = col_dev % cores
    same_core = [[x * cores + k for x in range(chips)] for k in range(cores)]
    transpose = [(r * grid + c, c * grid + r) for r in range(grid) for c in range(grid)]

    def by_half(x):
        return x.reshape(tokens, halves, BS).transpose(1, 0, 2)

    turned = lax.ppermute(activations, ("row", "col"), transpose)
    lead_piece = lax.all_to_all(
        by_half(activations).reshape(chips, part, BS), "col", 0, 0, axis_index_groups=same_core, tiled=True
    )[0]

    d0 = lax.reduce_precision(damping, 8, 7)
    d1 = lax.reduce_precision(damping - d0, 8, 7)
    d2 = damping - d0 - d1
    damp_rows = jnp.stack([d0, d1, d2, jnp.zeros_like(d2)]).astype(jnp.bfloat16).reshape(4 * halves, BS)
    pieces = to_all(jnp.concatenate([lead_piece, damp_rows]), "row", grid)
    damp = pieces[:PANELS, part:].reshape(PANELS, 4, width).astype(jnp.float32)
    damp = ((damp[:, 2] + damp[:, 1]) + damp[:, 0]).reshape(1, PANELS * width)

    own, pieces = lax.optimization_barrier((activations, pieces))
    sent = jnp.concatenate([pieces[:, :part].reshape(grid * part, BS), by_half(turned).reshape(halves * tokens, BS)])
    mine = to_all(sent, "col", chips, same_core)
    cols = lax.all_gather(own, "row")
    other = lax.ppermute(mine, "col", [(c, c ^ 1) for c in range(chips * cores)])
    at = jnp.stack([row_dev, col_dev, core]).astype(jnp.int32)
    return local_part(
        at, mine, other, cols, damp, damping.reshape(1, width), 1.0 / (tokens * grid), quarters
    )


def solution(mesh):
    in_specs = (P(("groups", "row"), "col"), P(("groups", "row")))
    out_specs = P(("groups", "row"), "col")
    return jax.shard_map(
        on_device, mesh=mesh, in_specs=in_specs, out_specs=out_specs, check_vma=False
    )
```

time: 163 us -> 181 us (1.11)
  the two profiles are of different devices: /device:TPU:65 before, /device:TPU:80 now
where the time goes in v2:
time: 181 us
  blocking collectives  74.6 us (41%)
  starting transfers between devices  54.4 us (30%)
  Pallas kernels  26.7 us (15%)
  waiting for transfers between devices  19.6 us (11%)
  local copies, waits for them, and re-layouts  3.47 us (2%)
  other arithmetic  1.94 us (1%)
    all_to_all x1, starting transfers between devices, to_all(): lax.all_to_all(shards, axis, 0, 0, axis_index_groups=groups, tiled=True)  43.7 us
    all_to_all x1, blocking collectives, to_all(): lax.all_to_all(shards, axis, 0, 0, axis_index_groups=groups, tiled=True)  40.5 us
    all_gather x1, blocking collectives, on_device(): cols = lax.all_gather(own, 'row')  34.1 us
    pallas_call x1, Pallas kernels, local_part(): pl.pallas_call(functools.partial(local_kernel, scale=scale, quarters=quar...  26.7 us
    all_to_all x1, waiting for transfers between devices, to_all(): lax.all_to_all(shards, axis, 0, 0, axis_index_groups=groups, tiled=True)  12.2 us
    all_to_all x1, waiting for transfers between devices, on_device(): lax.all_to_all(by_half(activations).reshape(chips, part, BS), 'col', 0, 0...  7.33 us
    all_to_all x1, starting transfers between devices, on_device(): lax.all_to_all(by_half(activations).reshape(chips, part, BS), 'col', 0, 0...  7.32 us
  transfers between devices with their start and end apart: 4, of which 2 were waited for; matrix products, arithmetic and copies ran while one was open for 1% of the time, Pallas kernels for 0%

profile of v2, /device:TPU:80, one launch (start us, length us, event | category | flops | bytes accessed | tf_op | source)
XLA Modules:
  0.0 180.8 jit_solution(16398303901845188489)
XLA Ops:
  0.0 0.8 reshape.54
  0.8 0.6 copy.5
  1.4 7.3 %all-to-all-start = ((bf16[8,24,128]{2,1,0:T(8,128)(2,1)}), bf16[8,24,128]{2,1,0:T(8,128)(2,1)S(1)}, u32[]{:S(2)}, u32[]{:S(2)}) async-start(bf16[8,24,128]{2,1,0:T(8,128)(2,1)} %bitcast.4), calls=%async_computation | async-start | bytes 98304 | tf_op jit(solution)/shard_map/all_to_all | solution.py:198
  8.8 0.7 reduce-precision_convert_fusion.1
  9.5 0.1 pad.7.clone
  9.5 0.1 maximum_maximum_fusion
  9.6 7.3 %all-to-all-done = bf16[8,24,128]{2,1,0:T(8,128)(2,1)S(1)} async-done(((bf16[8,24,128]{2,1,0:T(8,128)(2,1)}), bf16[8,24,128]{2,1,0:T(8,128)(2,1)S(1)}, u32[]{:S(2)}, u32[]{:S(2)}) %all-to-all-start) | async-done | bytes 49184 | tf_op jit(solution)/shard_map/all_to_all | solution.py:198
  17.0 0.7 broadcast_in_dim.6
  17.7 43.7 %all-to-all-start.1 = ((bf16[16,32,128]{2,1,0:T(8,128)(2,1)}), bf16[16,32,128]{2,1,0:T(8,128)(2,1)S(1)}, u32[]{:S(2)}, u32[]{:S(2)}) async-start(bf16[16,32,128]{2,1,0:T(8,128)(2,1)} %broadcast_in_dim.6), calls=%async_computation.1 | async-start | bytes 262144 | tf_op jit(solution)/shard_map/all_to_all | solution.py:177
  61.3 1.5 collective-permute-start
  62.8 0.0 collective-permute-done
  62.8 12.2 %all-to-all-done.1 = bf16[16,32,128]{2,1,0:T(8,128)(2,1)S(1)} async-done(((bf16[16,32,128]{2,1,0:T(8,128)(2,1)}), bf16[16,32,128]{2,1,0:T(8,128)(2,1)S(1)}, u32[]{:S(2)}, u32[]{:S(2)}) %all-to-all-start.1) | async-done | bytes 131104 | tf_op jit(solution)/shard_map/all_to_all | solution.py:177
  75.1 0.2 broadcast_in_dim.7
  75.3 0.0 copy-start.2
  75.3 40.5 %all_to_all.15.mine_ref = bf16[8,576,128]{2,1,0:T(8,128)(2,1)S(1)} all-to-all(bf16[8,576,128]{2,1,0:T(8,128)(2,1)S(1)} %broadcast_in_dim.7), channel_id=1, replica_groups={{0,2,4,6,8,10,12,14},{1,3,5,7,9,11,13,15},{16,18,20,22,24,26,28,30},{17..., dimensions={0} | all-to-all | bytes 2359296 | tf_op jit(solution)/shard_map/all_to_all | solution.py:177
  115.8 0.0 copy-start
  115.8 1.9 %collective-permute-start.1 = (bf16[8,576,128]{2,1,0:T(8,128)(2,1)S(1)}, bf16[8,576,128]{2,1,0:T(8,128)(2,1)S(1)}, u32[]{:S(2)}, u32[]{:S(2)}) collective-permute-start(bf16[8,576,128]{2,1,0:T(8,128)(2,1)S(1)} %all_to_all.15.mine_ref), channel_id=1, source_target_pairs={{0,1},{1,0},{2,3},{3,2},{4,5},{5,4},{6,7},{7,6},{8,9},{9,8},{10,11... | collective-permute-start | bytes 3538952 | tf_op jit(solution)/shard_map/ppermute | solution.py:214
  117.8 0.6 pad_add_fusion.at_ref
  118.4 0.6 slice_add_fusion
  118.9 0.0 copy-done.2
  118.9 34.1 %all-gather = bf16[1536,256]{1,0:T(8,128)(2,1)} all-gather(bf16[96,256]{1,0:T(8,128)(2,1)S(1)} %copy-done.2), channel_id=2, replica_groups=mesh['groups'=2,'row'=16,'col'=16] {'row'}, dimensions={0}, use_global_device_ids=true | all-gather | bytes 835584 | tf_op jit(solution)/shard_map/all_gather | solution.py:213
  153.0 0.0 collective-permute-done.1.other_ref
  153.0 0.0 copy-start.1
  153.0 0.0 copy-done
  153.1 1.0 copy-done.1
  154.1 26.7 %shard_map.28 = f32[256,256]{1,0:T(8,128)} custom-call(s32[3]{0:T(128)} %pad_add_fusion.at_ref, bf16[8,576,128]{2,1,0:T(8,128)(2,1)} %copy-done, bf16[8,576,128]{2,1,0:T(8,128)(2,1)} %copy-done.1, bf16[16,96,256]{2,1,0:T(8,128)(2,1)} %bitcast.14, f32[1,512]{1,0:T(1,128)} %bitcast.19, f32[1,256]{1,0:T(1,128)} %bitcast.20), custom_call_target="tpu_custom_call" | custom-call | tf_op jit(solution)/shard_map/pallas_call | solution.py:159
  (12 shorter events, 0.1 us)
Async XLA Ops:
  1.4 15.5 %all-to-all-start = ((bf16[8,24,128]{2,1,0:T(8,128)(2,1)}), bf16[8,24,128]{2,1,0:T(8,128)(2,1)S(1)}, u32[]{:S(2)}, u32[]{:S(2)}) async-start(bf16[8,24,128]{2,1,0:T(8,128)(2,1)} %bitcast.4), calls=%async_computation | async-start | bytes 98304 | tf_op jit(solution)/shard_map/all_to_all | solution.py:198
  17.7 57.4 %all-to-all-start.1 = ((bf16[16,32,128]{2,1,0:T(8,128)(2,1)}), bf16[16,32,128]{2,1,0:T(8,128)(2,1)S(1)}, u32[]{:S(2)}, u32[]{:S(2)}) async-start(bf16[16,32,128]{2,1,0:T(8,128)(2,1)} %broadcast_in_dim.6), calls=%async_computation.1 | async-start | bytes 262144 | tf_op jit(solution)/shard_map/all_to_all | solution.py:177
  61.3 1.5 collective-permute-start
  75.3 43.7 %copy-start.2 = (bf16[96,256]{1,0:T(8,128)(2,1)S(1)}, bf16[96,256]{1,0:T(8,128)(2,1)}, u32[]{:S(2)}) copy-start(bf16[96,256]{1,0:T(8,128)(2,1)} %param.2) | copy-start | bytes 147460
  115.8 37.3 %copy-start = (bf16[8,576,128]{2,1,0:T(8,128)(2,1)}, bf16[8,576,128]{2,1,0:T(8,128)(2,1)S(1)}, u32[]{:S(2)}) copy-start(bf16[8,576,128]{2,1,0:T(8,128)(2,1)S(1)} %all_to_all.15.mine_ref) | copy-start | bytes 3538948
  115.8 37.2 %collective-permute-start.1 = (bf16[8,576,128]{2,1,0:T(8,128)(2,1)S(1)}, bf16[8,576,128]{2,1,0:T(8,128)(2,1)S(1)}, u32[]{:S(2)}, u32[]{:S(2)}) collective-permute-start(bf16[8,576,128]{2,1,0:T(8,128)(2,1)S(1)} %all_to_all.15.mine_ref), channel_id=1, source_target_pairs={{0,1},{1,0},{2,3},{3,2},{4,5},{5,4},{6,7},{7,6},{8,9},{9,8},{10,11... | collective-permute-start | bytes 3538952 | tf_op jit(solution)/shard_map/ppermute | solution.py:214
  153.0 1.0 copy-start.1

commit v3 on v2

--- a/solution.py
+++ b/solution.py
@@ -27,37 +27,61 @@
     return jnp.concatenate([x, x], 1)
 
 
+def lanes(g, at):
+    return [jnp.broadcast_to(g[:, at + j : at + j + 1], (SUB, BS)) for j in range(SUB)]
+
+
+def sublane(x, m):
+    return jnp.broadcast_to(x[m : m + 1, :], (SUB, x.shape[1]))
+
+
 def factor_block(g_ref):
     sub = lax.broadcasted_iota(jnp.int32, (SUB, BS), 0)
     sub2 = lax.broadcasted_iota(jnp.int32, (SUB, 2 * BS), 0)
     strips = BS // SUB
+    half = strips // 2
     for k in range(strips):
         at = SUB * k
-        rows = g_ref[at : at + SUB, :]
-        cols = [jnp.broadcast_to(rows[:, at + j : at + j + 1], (SUB, BS)) for j in range(SUB)]
-        piv = [[jnp.broadcast_to(cols[j][m : m + 1, :], (SUB, BS)) for j in range(m + 1)] for m in range(SUB)]
+        end = (k // half + 1) * half
+        if k % half == 0:
+            if k > 0:
+                g_ref[at:, :] -= tdot(g_ref[:at, at:BS], g_ref[:at, :], HIGHEST)
+            rows = g_ref[at : at + SUB, :]
+            cols = lanes(rows, at)
+        ahead = k + 1 < end
+        if ahead:
+            next_rows = g_ref[at + SUB : at + 2 * SUB, :]
+            low = lanes(next_rows, at)
+            next_cols = lanes(next_rows, at + SUB)
         out = rows
         for j in range(SUB):
-            rc = 1.0 / piv[j][j]
-            rs = lax.rsqrt(piv[j][j])
-            t = {m: piv[m][j] * rc for m in range(j + 1, SUB)}
+            d = sublane(cols[j], j)
+            rc = 1.0 / d
+            rs = lax.rsqrt(d)
+            t = {m: sublane(cols[j], m) * rc for m in range(j + 1, SUB)}
+            if ahead:
+                for n in range(SUB):
+                    next_cols[n] = next_cols[n] - low[j] * (sublane(low[j], n) * rc)
+                for m in range(j + 1, SUB):
+                    low[m] = low[m] - low[j] * t[m]
             for m in range(j + 1, SUB):
-                for n in range(m, SUB):
-                    piv[n][m] = piv[n][m] - piv[n][j] * t[m]
                 cols[m] = jnp.where(sub == j, t[m], cols[m] - cols[j] * t[m])
-            row = jnp.broadcast_to(rows[j : j + 1, :], (SUB, 2 * BS))
+            row = sublane(rows, j)
             out = jnp.where(sub2 == j, row * both(rs), out)
             w = row * both(rc)
             rows = jnp.where(sub2 == j, w, rows - both(cols[j]) * w)
+            if ahead:
+                next_rows = next_rows - both(low[j]) * w
         g_ref[at : at + SUB, :] = out
-        if k + 1 < strips:
-            solved = [jnp.broadcast_to(rows[j : j + 1, :], (SUB, 2 * BS)) for j in range(SUB)]
-            for i in range(k + 1, strips):
-                g = g_ref[i * SUB : (i + 1) * SUB, :]
-                acc = g
-                for j in range(SUB):
-                    acc = acc - both(jnp.broadcast_to(g[:, at + j : at + j + 1], (SUB, BS))) * solved[j]
+        if k + 2 < end:
+            solved = [sublane(rows, j) for j in range(SUB)]
+            for i in range(k + 2, end):
+                acc = g_ref[i * SUB : (i + 1) * SUB, :]
+                for a, y in zip(lanes(acc, at), solved, strict=True):
+                    acc = acc - both(a) * y
                 g_ref[i * SUB : (i + 1) * SUB, :] = acc
+        if ahead:
+            rows, cols = next_rows, next_cols
 
 
 def local_kernel(
@@ -169,6 +193,7 @@
             pltpu.VMEM((LEAD, LEAD + 2 * NB), jnp.float32),
             pltpu.VMEM((BS, 2 * BS), jnp.float32),
         ],
+        compiler_params=pltpu.CompilerParams(vmem_limit_bytes=24 * 2**20),
     )(at, mine, other, cols, dlead, down)
 
 

time: 181 us -> 168 us (0.928)
  Pallas kernels: 26.7 us -> 18.4 us
  blocking collectives: 74.6 us -> 72.1 us
    pallas_call x1, Pallas kernels: 26.7 us -> 18.4 us  [local_part(): pl.pallas_call(functools.partial(local_kernel, scale=scale, quarters=quar...]
    all_gather x1, blocking collectives: 34.1 us -> 31.5 us  [on_device(): cols = lax.all_gather(own, 'row')]
where the time goes in v3:
time: 168 us
  blocking collectives  72.1 us (43%)
  starting transfers between devices  54.4 us (32%)
  waiting for transfers between devices  19.6 us (12%)
  Pallas kernels  18.4 us (11%)
  local copies, waits for them, and re-layouts  2.44 us (1%)
    all_to_all x1, starting transfers between devices, to_all(): lax.all_to_all(shards, axis, 0, 0, axis_index_groups=groups, tiled=True)  43.7 us
    all_to_all x1, blocking collectives, to_all(): lax.all_to_all(shards, axis, 0, 0, axis_index_groups=groups, tiled=True)  40.5 us
    all_gather x1, blocking collectives, on_device(): cols = lax.all_gather(own, 'row')  31.5 us
    pallas_call x1, Pallas kernels, local_part(): pl.pallas_call(functools.partial(local_kernel, scale=scale, quarters=quar...  18.4 us
    all_to_all x1, waiting for transfers between devices, to_all(): lax.all_to_all(shards, axis, 0, 0, axis_index_groups=groups, tiled=True)  12.2 us
    all_to_all x1, waiting for transfers between devices, on_device(): lax.all_to_all(by_half(activations).reshape(chips, part, BS), 'col', 0, 0...  7.33 us
    all_to_all x1, starting transfers between devices, on_device(): lax.all_to_all(by_half(activations).reshape(chips, part, BS), 'col', 0, 0...  7.32 us
  transfers between devices with their start and end apart: 4, of which 2 were waited for; matrix products, arithmetic and copies ran while one was open for 1% of the time, Pallas kernels for 0%

profile of v3, /device:TPU:80, one launch (start us, length us, event | category | flops | bytes accessed | tf_op | source)
XLA Modules:
  0.0 167.8 jit_solution(7882593062061327853)
XLA Ops:
  0.0 0.8 reshape.54
  0.8 0.6 copy.5
  1.4 7.3 %all-to-all-start = ((bf16[8,24,128]{2,1,0:T(8,128)(2,1)}), bf16[8,24,128]{2,1,0:T(8,128)(2,1)S(1)}, u32[]{:S(2)}, u32[]{:S(2)}) async-start(bf16[8,24,128]{2,1,0:T(8,128)(2,1)} %bitcast.4), calls=%async_computation | async-start | bytes 98304 | tf_op jit(solution)/shard_map/all_to_all | solution.py:223
  8.8 0.7 reduce-precision_convert_fusion.1
  9.5 0.1 pad.7.clone
  9.5 0.1 maximum_maximum_fusion
  9.6 7.3 %all-to-all-done = bf16[8,24,128]{2,1,0:T(8,128)(2,1)S(1)} async-done(((bf16[8,24,128]{2,1,0:T(8,128)(2,1)}), bf16[8,24,128]{2,1,0:T(8,128)(2,1)S(1)}, u32[]{:S(2)}, u32[]{:S(2)}) %all-to-all-start) | async-done | bytes 49184 | tf_op jit(solution)/shard_map/all_to_all | solution.py:223
  17.0 0.7 broadcast_in_dim.6
  17.7 43.7 %all-to-all-start.1 = ((bf16[16,32,128]{2,1,0:T(8,128)(2,1)}), bf16[16,32,128]{2,1,0:T(8,128)(2,1)S(1)}, u32[]{:S(2)}, u32[]{:S(2)}) async-start(bf16[16,32,128]{2,1,0:T(8,128)(2,1)} %broadcast_in_dim.6), calls=%async_computation.1 | async-start | bytes 262144 | tf_op jit(solution)/shard_map/all_to_all | solution.py:202
  61.3 1.5 collective-permute-start
  62.8 0.0 collective-permute-done
  62.8 12.2 %all-to-all-done.1 = bf16[16,32,128]{2,1,0:T(8,128)(2,1)S(1)} async-done(((bf16[16,32,128]{2,1,0:T(8,128)(2,1)}), bf16[16,32,128]{2,1,0:T(8,128)(2,1)S(1)}, u32[]{:S(2)}, u32[]{:S(2)}) %all-to-all-start.1) | async-done | bytes 131104 | tf_op jit(solution)/shard_map/all_to_all | solution.py:202
  75.1 0.2 broadcast_in_dim.7
  75.3 0.0 copy-start.1
  75.3 0.0 copy-start
  75.3 40.5 %all_to_all.15.mine_ref = bf16[8,576,128]{2,1,0:T(8,128)(2,1)S(1)} all-to-all(bf16[8,576,128]{2,1,0:T(8,128)(2,1)S(1)} %broadcast_in_dim.7), channel_id=1, replica_groups={{0,2,4,6,8,10,12,14},{1,3,5,7,9,11,13,15},{16,18,20,22,24,26,28,30},{17..., dimensions={0} | all-to-all | bytes 2359296 | tf_op jit(solution)/shard_map/all_to_all | solution.py:202
  115.8 1.9 %collective-permute-start.1 = (bf16[8,576,128]{2,1,0:T(8,128)(2,1)S(1)}, bf16[8,576,128]{2,1,0:T(8,128)(2,1)S(1)}, u32[]{:S(2)}, u32[]{:S(2)}) collective-permute-start(bf16[8,576,128]{2,1,0:T(8,128)(2,1)S(1)} %all_to_all.15.mine_ref), channel_id=1, source_target_pairs={{0,1},{1,0},{2,3},{3,2},{4,5},{5,4},{6,7},{7,6},{8,9},{9,8},{10,11... | collective-permute-start | bytes 3538952 | tf_op jit(solution)/shard_map/ppermute | solution.py:239
  117.8 0.1 pad_add_fusion.at_ref
  117.9 0.0 copy-done.1
  117.9 31.5 %all-gather = bf16[1536,256]{1,0:T(8,128)(2,1)S(1)} all-gather(bf16[96,256]{1,0:T(8,128)(2,1)S(1)} %copy-done.1), channel_id=2, replica_groups=mesh['groups'=2,'row'=16,'col'=16] {'row'}, dimensions={0}, use_global_device_ids=true | all-gather | bytes 835584 | tf_op jit(solution)/shard_map/all_gather | solution.py:238
  149.4 0.0 collective-permute-done.1.other_ref
  149.4 0.0 copy-done
  149.4 18.4 %shard_map.28 = f32[256,256]{1,0:T(8,128)} custom-call(s32[3]{0:T(128)S(1)} %pad_add_fusion.at_ref, bf16[8,576,128]{2,1,0:T(8,128)(2,1)S(1)} %all_to_all.15.mine_ref, bf16[8,576,128]{2,1,0:T(8,128)(2,1)S(1)} %collective-permute-done.1.other_ref, bf16[16,96,256]{2,1,0:T(8,128)(2,1)S(1)} %bitcast.14, f32[1,512]{1,0:T(1,128)S(1)} %bitcast.15, f32[1,256]{1,0:T(1,128)S(1)} %bitcast.16), custom_call_target="tpu_custom_call" | custom-call | tf_op jit(solution)/shard_map/pallas_call | solution.py:183
  (13 shorter events, 0.1 us)
Async XLA Ops:
  1.4 15.5 %all-to-all-start = ((bf16[8,24,128]{2,1,0:T(8,128)(2,1)}), bf16[8,24,128]{2,1,0:T(8,128)(2,1)S(1)}, u32[]{:S(2)}, u32[]{:S(2)}) async-start(bf16[8,24,128]{2,1,0:T(8,128)(2,1)} %bitcast.4), calls=%async_computation | async-start | bytes 98304 | tf_op jit(solution)/shard_map/all_to_all | solution.py:223
  17.7 57.4 %all-to-all-start.1 = ((bf16[16,32,128]{2,1,0:T(8,128)(2,1)}), bf16[16,32,128]{2,1,0:T(8,128)(2,1)S(1)}, u32[]{:S(2)}, u32[]{:S(2)}) async-start(bf16[16,32,128]{2,1,0:T(8,128)(2,1)} %broadcast_in_dim.6), calls=%async_computation.1 | async-start | bytes 262144 | tf_op jit(solution)/shard_map/all_to_all | solution.py:202
  61.3 1.5 collective-permute-start
  75.3 42.6 %copy-start.1 = (bf16[96,256]{1,0:T(8,128)(2,1)S(1)}, bf16[96,256]{1,0:T(8,128)(2,1)}, u32[]{:S(2)}) copy-start(bf16[96,256]{1,0:T(8,128)(2,1)} %param.2) | copy-start | bytes 147460
  75.3 74.1 %copy-start = (f32[256]{0:T(256)S(1)}, f32[256]{0:T(256)}, u32[]{:S(2)}) copy-start(f32[256]{0:T(256)} %param.3) | copy-start | bytes 3076
  115.8 33.6 %collective-permute-start.1 = (bf16[8,576,128]{2,1,0:T(8,128)(2,1)S(1)}, bf16[8,576,128]{2,1,0:T(8,128)(2,1)S(1)}, u32[]{:S(2)}, u32[]{:S(2)}) collective-permute-start(bf16[8,576,128]{2,1,0:T(8,128)(2,1)S(1)} %all_to_all.15.mine_ref), channel_id=1, source_target_pairs={{0,1},{1,0},{2,3},{3,2},{4,5},{5,4},{6,7},{7,6},{8,9},{9,8},{10,11... | collective-permute-start | bytes 3538952 | tf_op jit(solution)/shard_map/ppermute | solution.py:239
